TPU v7x, 128 devices: a whole 4x4x4 slice. The times are simulated.
128 devices in a mesh: grp: 64 (over z, y, x), loc: 2 (over core).
Axes of the slice: x: 4, y: 4, z: 4, core: 2. Of those that a mesh axis runs over, the one named last changes fastest.
Arguments:
- tokens: bfloat16 [4096, 3584], P(('grp', 'loc')), may hold values from -6 to 6
- gate_weights: bfloat16 [4096, 8], P(('grp', 'loc')), may hold values from 0.099609375 to 0.59765625
- expert_ids: int32 [4096, 8], P(('grp', 'loc')), may hold values from 0 to 127, as said below
- w_gate: bfloat16 [128, 3584, 1024], P('grp', None, 'loc'), may hold values from -0.09375 to 0.09375
- w_up: bfloat16 [128, 3584, 1024], P('grp', None, 'loc'), may hold values from -0.09375 to 0.09375
- w_down: bfloat16 [128, 3584, 1024], P('grp', None, 'loc'), may hold values from -0.1875 to 0.1875
Outputs:
- layer_out: bfloat16 [4096, 3584], P(('grp', 'loc'))
Inputs may be any that keep to these rules, and one draw needn't show every extreme that they name: `expert_ids`: each row names 8 different experts: two in each of 4 different routing groups, a routing group being 16 consecutive expert numbers. Among the rows of one device (aligned blocks of 32 rows) each expert is named at most 4 times, and in every such block some expert is named exactly 4 times.
All inputs are finite; a program needn't handle non-finite values.
Results may differ from a plain program's by a relative error of at most 0.01.
Values may be sent and summed in bfloat16 or wider, within the bound.
A program may use at most 192 MiB of HBM per device.

v0:
```python
import jax
import jax.numpy as jnp
from jax import lax
from jax.sharding import PartitionSpec as P

RGROUPS = 8


def expert_rows(inputs, scales, gate_part, up_part, down_part):
    gate_act = jnp.dot(inputs, gate_part, preferred_element_type=jnp.float32)
    upward = jnp.dot(inputs, up_part, preferred_element_type=jnp.float32)
    hidden = (jax.nn.silu(gate_act) * upward).astype(jnp.bfloat16)
    projected = lax.dot_general(
        hidden, down_part, (((1,), (1,)), ((), ())), preferred_element_type=jnp.float32
    )
    return projected * scales.astype(jnp.float32)[:, None]


def weights_path(rows_in, scales_in, w_gate, w_up, w_down):
    row_dims = rows_in.shape
    shard_units = w_gate.shape[2]
    expert_inputs = [rows_in[:, expert].reshape(-1, row_dims[3]) for expert in range(row_dims[1])]
    expert_scales = [scales_in[:, expert].reshape(-1) for expert in range(row_dims[1])]
    starting = tuple(
        (
            jnp.zeros((row_dims[0] * row_dims[2], row_dims[3]), jnp.float32)
            for expert in range(row_dims[1])
        )
    )
    gate_piece = lax.all_gather(w_gate, "loc", axis=2, tiled=True)
    up_piece = lax.all_gather(w_up, "loc", axis=2, tiled=True)
    down_piece = lax.all_gather(w_down, "loc", axis=2, tiled=True)
    updated = []
    for expert in range(row_dims[1]):
        running = starting[expert]
        for block_index in range(gate_piece.shape[2] // shard_units):
            lower_unit = block_index * shard_units
            upper_unit = lower_unit + shard_units
            values = expert_rows(
                expert_inputs[expert],
                expert_scales[expert],
                gate_piece[expert][:, lower_unit:upper_unit],
                up_piece[expert][:, lower_unit:upper_unit],
                down_piece[expert][:, lower_unit:upper_unit],
            )
            rounded = lax.optimization_barrier(values.astype(jnp.bfloat16))
            running = running + rounded.astype(jnp.float32)
        updated.append(running)
    folded = tuple(updated)
    stacked = jnp.stack(
        [folded_part.reshape(row_dims[0], row_dims[2], row_dims[3]) for folded_part in folded],
        axis=1,
    )
    return stacked.astype(jnp.bfloat16)


def body(tokens, gate_weights, expert_ids, w_gate, w_up, w_down):
    tok_count = tokens.shape[0]
    choices_per = expert_ids.shape[1]
    feature_count = tokens.shape[1]
    group_count = lax.axis_size("grp")
    local_experts = w_gate.shape[0]
    expert_total = group_count * local_experts
    slot_depth = 2 * tok_count * RGROUPS // expert_total
    slot_total = expert_total * slot_depth
    pair_ids = expert_ids.reshape(-1)
    pair_count = pair_ids.shape[0]
    pair_order = jnp.arange(pair_count, dtype=jnp.int32)
    same_expert = (pair_ids[:, None] == pair_ids[None, :]).astype(jnp.int32)
    earlier = (pair_order[:, None] > pair_order[None, :]).astype(jnp.int32)
    slot_rank = jnp.sum(same_expert * earlier, axis=1)
    position = pair_ids * slot_depth + slot_rank
    pair_onehot = jnp.arange(slot_total, dtype=jnp.int32)[:, None] == position[None, :]
    placement = jnp.sum(
        pair_onehot.reshape(slot_total, tok_count, choices_per).astype(jnp.int32), axis=2
    ).astype(jnp.bfloat16)
    send_rows = jnp.dot(placement, tokens, preferred_element_type=jnp.float32).astype(jnp.bfloat16)
    flat_scales = gate_weights.reshape(-1).astype(jnp.float32)
    send_scales = jnp.sum(jnp.where(pair_onehot, flat_scales[None, :], 0.0), axis=1).astype(
        jnp.bfloat16
    )
    send_rows = send_rows.reshape(group_count, local_experts, slot_depth, feature_count)
    send_scales = send_scales.reshape(group_count, local_experts, slot_depth)
    computed = weights_path(
        lax.all_to_all(send_rows, "grp", split_axis=0, concat_axis=0, tiled=True),
        lax.all_to_all(send_scales, "grp", split_axis=0, concat_axis=0, tiled=True),
        w_gate,
        w_up,
        w_down,
    )
    returned = lax.all_to_all(computed, "grp", split_axis=0, concat_axis=0, tiled=True)
    flat_back = returned.reshape(slot_total, feature_count)
    mixed_out = lax.dot_general(
        placement, flat_back, (((0,), (0,)), ((), ())), preferred_element_type=jnp.float32
    )
    return mixed_out.astype(jnp.bfloat16)


def solution(mesh):
    placed = (
        P(("grp", "loc"), None),
        P(("grp", "loc"), None),
        P(("grp", "loc"), None),
        P("grp", None, "loc"),
        P("grp", None, "loc"),
        P("grp", None, "loc"),
    )
    return jax.shard_map(
        body, mesh=mesh, in_specs=placed, out_specs=P(("grp", "loc"), None), check_vma=False
    )
```

profile of v0, /device:TPU:1, one launch (start us, length us, event | category | flops | bytes accessed | tf_op | source)
XLA Modules:
  0.0 254.1 jit_solution(14169747919232399582)
XLA Ops:
  10.2 12.0 %all-to-all-start.1 = ((bf16[64,2,4]{2,1,0:T(2,128)(2,1)}), bf16[64,2,4]{2,1,0:T(2,128)(2,1)S(1)}, u32[]{:S(2)}, u32[]{:S(2)}) async-start(bf16[64,2,4]{2,1,0:T(2,128)(2,1)} %convert_element_type.100), calls=%async_computation.1 | async-start | bytes 65536 | tf_op jit(solution)/shard_map/all_to_all | solution.py:86
  22.5 3.7 %convolution_convert_fusion = bf16[512,3584]{1,0:T(8,128)(2,1)} fusion(bf16[32,3584]{1,0:T(8,128)(2,1)S(1)} %copy-done, s32[512,32]{0,1:T(8,128)S(1)} %convert_reduce_fusion), kind=kOutput, calls=%fused_computation.6 | convolution fusion | flops 119291904 | bytes 3964928 | tf_op jit(solution)/shard_map/dot_general | solution.py:77
  26.3 7.4 %reshape.52 = bf16[64,2,4,3584]{3,2,1,0:T(4,128)(2,1)} reshape(bf16[512,3584]{1,0:T(8,128)(2,1)} %convolution_convert_fusion) | data formatting | bytes 7340032 | tf_op jit(solution)/shard_map/reshape | solution.py:82
  33.6 10.4 %all-to-all-start = ((bf16[64,2,4,3584]{3,2,1,0:T(4,128)(2,1)}), bf16[64,2,4,3584]{3,2,1,0:T(4,128)(2,1)}, u32[]{:S(2)}, u32[]{:S(2)}) async-start(bf16[64,2,4,3584]{3,2,1,0:T(4,128)(2,1)} %reshape.52), calls=%async_computation | async-start | bytes 7340032 | tf_op jit(solution)/shard_map/all_to_all | solution.py:85
  44.4 44.4 %all-to-all-done = bf16[64,2,4,3584]{3,2,1,0:T(4,128)(2,1)} async-done(((bf16[64,2,4,3584]{3,2,1,0:T(4,128)(2,1)}), bf16[64,2,4,3584]{3,2,1,0:T(4,128)(2,1)}, u32[]{:S(2)}, u32[]{:S(2)}) %all-to-all-start) | async-done | bytes 3670048 | tf_op jit(solution)/shard_map/all_to_all | solution.py:85
  88.9 5.8 %fusion.88 = (bf16[64,1,4,3584]{3,2,1,0:T(4,128)(2,1)}, bf16[64,1,4,3584]{3,2,1,0:T(4,128)(2,1)S(1)}) fusion(bf16[64,2,4,3584]{3,2,1,0:T(4,128)(2,1)} %all-to-all-done), kind=kLoop, calls=%fused_computation.89 | loop fusion | bytes 7340032 | tf_op jit(solution)/shard_map/slice | solution.py:22
  94.6 4.3 %reshape_squeeze.8 = bf16[256,3584]{1,0:T(8,128)(2,1)} reshape(bf16[64,1,4,3584]{3,2,1,0:T(4,128)(2,1)} %get-tuple-element.13) | data formatting | bytes 3670016 | tf_op jit(solution)/shard_map/reshape;squeeze | solution.py:22
  100.4 6.5 %slice_bitcast_fusion.5 = (bf16[3584,1024]{1,0:T(8,128)(2,1)S(1)}, bf16[3584,1024]{1,0:T(8,128)(2,1)S(1)}) fusion(bf16[2,3584,1024]{2,1,0:T(8,128)(2,1)} %all-gather.4.cloned.1.call-done), kind=kLoop, calls=%fused_computation.5 | loop fusion | bytes 29360128 | tf_op jit(solution)/shard_map/squeeze | solution.py:42
  106.9 1.9 fusion.17
  108.8 1.9 fusion.22
  113.0 10.6 %slice_bitcast_fusion.4 = (bf16[3584,1024]{1,0:T(8,128)(2,1)}, bf16[3584,1024]{1,0:T(8,128)(2,1)}) fusion(bf16[2,3584,1024]{2,1,0:T(8,128)(2,1)} %all-gather.6.cloned.1.call-done), kind=kLoop, calls=%fused_computation.4 | loop fusion | bytes 29360128 | tf_op jit(solution)/shard_map/squeeze | solution.py:43
  123.6 10.5 %slice_bitcast_fusion.3 = (bf16[3584,1024]{1,0:T(8,128)(2,1)}, bf16[3584,1024]{1,0:T(8,128)(2,1)}) fusion(bf16[2,3584,1024]{2,1,0:T(8,128)(2,1)} %all-gather.8.cloned.1.call-done), kind=kLoop, calls=%fused_computation.3 | loop fusion | bytes 29360128 | tf_op jit(solution)/shard_map/squeeze | solution.py:44
  134.1 6.9 %fusion = bf16[256,3584]{1,0:T(8,128)(2,1)} fusion(bf16[3584,1024]{1,0:T(8,128)(2,1)} %get-tuple-element.11, f32[256]{0:T(256)S(1)} %reshape.55, bf16[256,3584]{1,0:T(8,128)(2,1)S(1)} %copy-done.3, bf16[3584,1024]{1,0:T(8,128)(2,1)} %get-tuple-element.9, f32[256,512]{1,0:T(8,128)} %fusion.22), kind=kOutput, calls=%fused_computation.11 | convolution fusion | flops 1881669632 | bytes 11535360 | tf_op jit(solution)/shard_map/dot_general | solution.py:13
  141.0 6.8 %fusion.1 = bf16[256,3584]{1,0:T(8,128)(2,1)} fusion(bf16[3584,1024]{1,0:T(8,128)(2,1)} %get-tuple-element.11, f32[256]{0:T(256)S(1)} %reshape.55, bf16[256,3584]{1,0:T(8,128)(2,1)S(1)} %copy-done.3, bf16[3584,1024]{1,0:T(8,128)(2,1)} %get-tuple-element.9, f32[256,512]{1,0:T(8,128)} %fusion.17), kind=kOutput, calls=%fused_computation.12 | convolution fusion | flops 1881669632 | bytes 11535360 | tf_op jit(solution)/shard_map/dot_general | solution.py:13
  147.8 3.7 %add_convert_fusion.1 = bf16[256,3584]{1,0:T(8,128)(2,1)} fusion(bf16[256,3584]{1,0:T(8,128)(2,1)} %fusion.1, bf16[256,3584]{1,0:T(8,128)(2,1)} %fusion), kind=kLoop, calls=%fused_computation.38 | loop fusion | flops 3670016 | bytes 5505024 | tf_op jit(solution)/shard_map/convert.6
  151.5 3.3 %stack_reshape.8 = bf16[64,1,4,3584]{3,2,0,1:T(4,128)(2,1)S(1)} reshape(bf16[256,3584]{1,0:T(8,128)(2,1)} %add_convert_fusion.1) | data formatting | bytes 3670016 | tf_op jit(solution)/shard_map/stack;reshape | solution.py:50
  154.9 7.1 %fusion.2 = bf16[256,3584]{1,0:T(8,128)(2,1)} fusion(bf16[3584,1024]{1,0:T(8,128)(2,1)} %get-tuple-element.12, f32[256]{0:T(256)S(1)} %reshape.56, bf16[256,3584]{1,0:T(8,128)(2,1)} %reshape_squeeze.9, bf16[3584,1024]{1,0:T(8,128)(2,1)} %get-tuple-element.10, f32[256,512]{1,0:T(8,128)S(1)} %fusion.12), kind=kOutput, calls=%fused_computation.13 | convolution fusion | flops 1881669632 | bytes 11535360 | tf_op jit(solution)/shard_map/dot_general | solution.py:13
  162.0 7.2 %fusion.3 = bf16[256,3584]{1,0:T(8,128)(2,1)} fusion(bf16[3584,1024]{1,0:T(8,128)(2,1)} %get-tuple-element.12, f32[256]{0:T(256)S(1)} %reshape.56, bf16[256,3584]{1,0:T(8,128)(2,1)} %reshape_squeeze.9, bf16[3584,1024]{1,0:T(8,128)(2,1)} %get-tuple-element.10, f32[256,512]{1,0:T(8,128)S(1)} %fusion.7), kind=kOutput, calls=%fused_computation.14 | convolution fusion | flops 1881669632 | bytes 11535360 | tf_op jit(solution)/shard_map/dot_general | solution.py:13
  169.2 3.8 %add_convert_fusion = bf16[256,3584]{1,0:T(8,128)(2,1)} fusion(bf16[256,3584]{1,0:T(8,128)(2,1)} %fusion.3, bf16[256,3584]{1,0:T(8,128)(2,1)} %fusion.2), kind=kLoop, calls=%fused_computation.37 | loop fusion | flops 3670016 | bytes 5505024 | tf_op jit(solution)/shard_map/convert.5
  173.0 4.1 %stack_reshape.9 = bf16[64,1,4,3584]{3,2,0,1:T(4,128)(2,1)} reshape(bf16[256,3584]{1,0:T(8,128)(2,1)} %add_convert_fusion) | data formatting | bytes 3670016 | tf_op jit(solution)/shard_map/stack;reshape | solution.py:50
  177.1 3.9 %pad_maximum_fusion = bf16[64,2,4,3584]{3,2,1,0:T(4,128)(2,1)S(1)} fusion(bf16[64,1,4,3584]{3,2,1,0:T(4,128)(2,1)} %bitcast.25, bf16[64,1,4,3584]{3,2,1,0:T(4,128)(2,1)S(1)} %bitcast.24), kind=kLoop, calls=%fused_computation.36 | loop fusion | flops 1835008 | bytes 7340032 | tf_op jit(solution)/shard_map/stack | solution.py:50
  181.1 56.3 %all_to_all.15 = bf16[64,2,4,3584]{3,2,1,0:T(4,128)(2,1)} all-to-all(bf16[64,2,4,3584]{3,2,1,0:T(4,128)(2,1)S(1)} %pad_maximum_fusion), channel_id=1, replica_groups=mesh['grp'=64,'loc'=2] {'grp'}, dimensions={0} | all-to-all | bytes 7340032 | tf_op jit(solution)/shard_map/all_to_all | solution.py:91
  237.3 6.8 %reshape.53 = bf16[512,3584]{1,0:T(8,128)(2,1)} reshape(bf16[64,2,4,3584]{3,2,1,0:T(4,128)(2,1)} %all_to_all.15) | data formatting | bytes 7340032 | tf_op jit(solution)/shard_map/reshape | solution.py:92
  244.1 3.5 %convolution_convert_fusion.1 = bf16[32,3584]{1,0:T(8,128)(2,1)} fusion(bf16[512,3584]{1,0:T(8,128)(2,1)} %reshape.53, s32[512,32]{0,1:T(8,128)S(1)} %convert_reduce_fusion), kind=kOutput, calls=%fused_computation.15 | convolution fusion | flops 117571584 | bytes 3964928 | tf_op jit(solution)/shard_map/dot_general | solution.py:93
  (39 shorter events, 8.0 us)
Async XLA Ops:
  6.5 16.0 %copy-start = (bf16[32,3584]{1,0:T(8,128)(2,1)S(1)}, bf16[32,3584]{1,0:T(8,128)(2,1)}, u32[]{:S(2)}) copy-start(bf16[32,3584]{1,0:T(8,128)(2,1)} %param.6) | copy-start | bytes 688132
  6.5 93.9 %all-gather.4.cloned.1.call-start = ((), (), s32[]{:S(2)}) async-start(), calls=%async_computation.3 | async-start | bytes 22020096 | tf_op jit(solution)/shard_map/all_gather | solution.py:30
  7.3 105.7 %all-gather.6.cloned.1.call-start = ((), (), s32[]{:S(2)}) async-start(), calls=%async_computation.4 | async-start | bytes 22020096 | tf_op jit(solution)/shard_map/all_gather | solution.py:31
  8.0 0.8 copy-start.4
  8.0 0.9 copy-start.5
  8.0 115.6 %all-gather.8.cloned.1.call-start = ((), (), s32[]{:S(2)}) async-start(), calls=%async_computation.5 | async-start | bytes 22020096 | tf_op jit(solution)/shard_map/all_gather | solution.py:32
  10.2 23.4 %all-to-all-start.1 = ((bf16[64,2,4]{2,1,0:T(2,128)(2,1)}), bf16[64,2,4]{2,1,0:T(2,128)(2,1)S(1)}, u32[]{:S(2)}, u32[]{:S(2)}) async-start(bf16[64,2,4]{2,1,0:T(2,128)(2,1)} %convert_element_type.100), calls=%async_computation.1 | async-start | bytes 65536 | tf_op jit(solution)/shard_map/all_to_all | solution.py:86
  33.6 55.2 %all-to-all-start = ((bf16[64,2,4,3584]{3,2,1,0:T(4,128)(2,1)}), bf16[64,2,4,3584]{3,2,1,0:T(4,128)(2,1)}, u32[]{:S(2)}, u32[]{:S(2)}) async-start(bf16[64,2,4,3584]{3,2,1,0:T(4,128)(2,1)} %reshape.52), calls=%async_computation | async-start | bytes 7340032 | tf_op jit(solution)/shard_map/all_to_all | solution.py:85
  100.4 6.5 %copy-start.3 = (bf16[256,3584]{1,0:T(8,128)(2,1)S(1)}, bf16[256,3584]{1,0:T(8,128)(2,1)}, u32[]{:S(2)}) copy-start(bf16[256,3584]{1,0:T(8,128)(2,1)} %reshape_squeeze.8) | copy-start | bytes 5505028
  108.8 1.9 copy-start.2
  237.3 10.3 %copy-start.1 = (bf16[32,3584]{1,0:T(8,128)(2,1)S(1)}, bf16[32,3584]{1,0:T(8,128)(2,1)}, u32[]{:S(2)}) copy-start(bf16[32,3584]{1,0:T(8,128)(2,1)} %param.6) | copy-start | bytes 688132
Sparse Core Ops, SparseCore 0:
  9.0 33.3 all-gather.3
  44.1 31.0 all-gather.5
  76.8 31.0 all-gather.7
where the time goes:
time: 255 us; the launch traced here: 254 us
  local copies, waits for them, and re-layouts  62.1 us (24%)
  blocking collectives  56.3 us (22%)
  waiting for transfers between devices  46.5 us (18%)
  matrix products  41.3 us (16%)
  starting transfers between devices  22.4 us (9%)
  between operations  13.3 us (5%)
  other arithmetic  12.2 us (5%)
    all_to_all x1, blocking collectives, body(): lax.all_to_all(computed, 'grp', split_axis=0, concat_axis=0, tiled=True)  56.3 us
    all_to_all x1, waiting for transfers between devices, body(): lax.all_to_all(send_rows, 'grp', split_axis=0, concat_axis=0, tiled=True)  44.4 us
    dot_general x4, matrix products, expert_rows(): lax.dot_general(hidden, down_part, (((1,), (1,)), ((), ())), preferred_el...  28 us
    all_to_all x1, starting transfers between devices, body(): lax.all_to_all(send_scales, 'grp', split_axis=0, concat_axis=0, tiled=True)  12 us
    squeeze x1, local copies, waits for them, and re-layouts, weights_path(): up_piece[expert][:, lower_unit:upper_unit]  10.6 us
    squeeze x1, local copies, waits for them, and re-layouts, weights_path(): down_piece[expert][:, lower_unit:upper_unit]  10.5 us
    all_to_all x1, starting transfers between devices, body(): lax.all_to_all(send_rows, 'grp', split_axis=0, concat_axis=0, tiled=True)  10.4 us
    another operation x2, other arithmetic  7.54 us
  transfers between devices with their start and end apart: 5, of which 1 were waited for; matrix products, arithmetic and copies ran while one was open for 19% of the time, Pallas kernels for 0%

commit v1 on v0

v1 whole, which is shorter than its diff:
```python
import jax
import jax.numpy as jnp
from jax import lax
from jax.experimental import pallas as pl
from jax.experimental.pallas import tpu as pltpu
from jax.sharding import PartitionSpec as P

SIDE = 4
CUBE = 8
MOST = 4
STEP = 512
LAG_IN = 2
LAG_BACK = 3
LAG_SUM = 5
F32 = jnp.float32
BF16 = jnp.bfloat16


def paired(coord, kind):
    odd = lax.rem(coord + kind, 2)
    return lax.rem(coord + SIDE + 1 - 2 * odd, SIDE)


def cube_of(place, kind):
    pairs = [(coord, paired(coord, kind)) for coord in place]
    return [
        (pairs[0][d // 4] * SIDE + pairs[1][d // 2 % 2]) * SIDE + pairs[2][d % 2]
        for d in range(CUBE)
    ]


def dot(left, right):
    return jnp.dot(left, right, preferred_element_type=F32)


def kernel(
    tokens, scales, ids, w_gate, w_up, w_down, out,
    held, table, pick, mix, sent, rows, gate_acc, up_acc, hidden, made, back, part, last,
    gate_v, up_v, down_v,
    tok_sem, table_sems, s1, s2, s3, s4, w_local, w_send, w_recv,
):
    count = tokens.shape[0]
    steps = held.shape[0]
    block = CUBE * MOST
    slots = 2 * CUBE * block
    me = lax.axis_index("grp")
    core = lax.axis_index("loc")
    other = 1 - core
    place = (me // (SIDE * SIDE), lax.rem(me // SIDE, SIDE), lax.rem(me, SIDE))
    near = cube_of(place, core)
    far = cube_of(place, other)

    def feature_span(step):
        return pl.ds(pl.multiple_of(step * STEP, STEP), STEP)

    def token_load(step):
        return pltpu.make_async_copy(
            tokens.at[:, feature_span(step)], held.at[step, pl.ds(0, count)], tok_sem.at[step]
        )

    def weight_load(which, step):
        source = (w_gate, w_up, w_down)[which]
        target = (gate_v, up_v, down_v)[which]
        return pltpu.make_async_copy(
            source.at[core, feature_span(step)], target.at[step, 0], w_local.at[which, step]
        )

    def weight_send(which, step):
        source = (w_gate, w_up, w_down)[which]
        target = (gate_v, up_v, down_v)[which]
        return pltpu.make_async_remote_copy(
            src_ref=source.at[other, feature_span(step)],
            dst_ref=target.at[step, 1],
            send_sem=w_send.at[which, step],
            recv_sem=w_recv.at[which, step],
            device_id={"grp": me, "loc": other},
            device_id_type=pl.DeviceIdType.MESH,
        )

    def send(source, target, sems, chip, to_core):
        pltpu.make_async_remote_copy(
            src_ref=source,
            dst_ref=target,
            send_sem=sems[0],
            recv_sem=sems[1],
            device_id={"grp": chip, "loc": to_core},
            device_id_type=pl.DeviceIdType.MESH,
        ).start()

    def wait_for(ref, sem):
        pltpu.make_async_copy(ref, ref, sem).wait()

    for step in range(steps):
        token_load(step).start()
    barrier = pltpu.get_barrier_semaphore()
    partners = [(me, other)]
    for d in range(1, CUBE):
        partners += [(near[d], core), (near[d], other), (far[d], core), (far[d], other)]
    for chip, to_core in partners:
        pl.semaphore_signal(
            barrier, inc=1, device_id={"grp": chip, "loc": to_core},
            device_id_type=pl.DeviceIdType.MESH,
        )

    def start_weights(step, carry):
        for which in range(3):
            weight_load(which, step).start()
        return carry

    lax.fori_loop(0, steps, start_weights, 0)

    expert_line = lax.broadcasted_iota(jnp.int32, (count, 128), 1)
    chosen = jnp.zeros((count, 128), F32)
    weight_of = jnp.zeros((count, 128), F32)
    for k in range(ids.shape[1]):
        match = ids[:, k : k + 1] == expert_line
        chosen = chosen + jnp.where(match, 1.0, 0.0)
        weight_of = weight_of + jnp.where(match, scales[:, k : k + 1].astype(F32), 0.0)
    before = (
        lax.broadcasted_iota(jnp.int32, (count, count), 1)
        < lax.broadcasted_iota(jnp.int32, (count, count), 0)
    )
    earlier = dot(jnp.where(before, 1.0, 0.0).astype(BF16), chosen.astype(BF16))
    table[0, :count] = (chosen * (earlier + 1.0)).astype(BF16)
    table[0, count:] = weight_of.astype(BF16)
    gate_acc[...] = jnp.zeros_like(gate_acc)
    up_acc[...] = jnp.zeros_like(up_acc)

    pl.semaphore_wait(barrier, len(partners))

    for d in range(1, CUBE):
        send(table.at[0], table.at[d], (table_sems.at[0], table_sems.at[1]), near[d], core)

    def spread(step, carry):
        token_load(step).wait()
        for d in range(1, CUBE):
            send(
                held.at[step, pl.ds(0, count)], held.at[step, pl.ds(d * count, count)],
                (s1.at[0, step], s1.at[1, step]), near[d], core,
            )
        return carry

    lax.fori_loop(0, steps, spread, 0)

    slot = lax.broadcasted_iota(jnp.int32, (1, slots), 1)
    slot_core = slot // (CUBE * block)
    slot_chip = slot // block % CUBE
    slot_source = slot // MOST % CUBE
    slot_rank = slot % MOST
    pairs = [(coord, paired(coord, other)) for coord in place]
    chip = (
        jnp.where(slot_chip // 4 == 0, pairs[0][0], pairs[0][1]) * SIDE
        + jnp.where(slot_chip // 2 % 2 == 0, pairs[1][0], pairs[1][1])
    ) * SIDE + jnp.where(slot_chip % 2 == 0, pairs[2][0], pairs[2][1])
    slot_expert = chip * 2 + (core + slot_core) % 2
    widen = jnp.where(
        lax.broadcasted_iota(jnp.int32, (128, slots), 0) == slot_expert, 1.0, 0.0
    ).astype(BF16)

    wait_for(table.at[pl.ds(1, CUBE - 1)], table_sems.at[1])
    codes = jnp.concatenate([table[d, :count] for d in range(CUBE)], axis=0)
    weights = jnp.concatenate([table[d, count:] for d in range(CUBE)], axis=0)
    token_source = lax.broadcasted_iota(jnp.int32, (CUBE * count, 1), 0) // count
    hit = (dot(codes, widen) == (slot_rank + 1).astype(F32)) & (token_source == slot_source)
    mix[...] = jnp.where(hit, dot(weights, widen), 0.0).astype(BF16)
    pick[...] = jnp.where(hit, 1.0, 0.0).T.astype(BF16)

    def select(step):
        wait_for(held.at[step, pl.ds(count, (CUBE - 1) * count)], s1.at[1, step])
        chosen_rows = dot(pick[...], held[step]).astype(BF16)
        sent[step] = chosen_rows
        rows[step, :block] = chosen_rows[:block]
        for across in range(2):
            for d in range(CUBE):
                if across + d > 0:
                    span = pl.ds((across * CUBE + d) * block, block)
                    send(
                        sent.at[step, span], rows.at[step, span], (s2.at[0, step], s2.at[1, step]),
                        far[d], other if across else core,
                    )
        for which in range(3):
            weight_send(which, step).start()

    def accumulate(step):
        for which in range(2):
            weight_load(which, step).wait()
            weight_send(which, step).wait_recv()
        wait_for(rows.at[step, pl.ds(block, slots - block)], s2.at[1, step])
        arrived = rows[step]
        half = gate_v.shape[3]
        for h in range(2):
            gate_acc[:, h * half : (h + 1) * half] += dot(arrived, gate_v[step, h])
            up_acc[:, h * half : (h + 1) * half] += dot(arrived, up_v[step, h])

    def inward(turn, carry):
        @pl.when(turn < steps)
        def _():
            select(turn)

        @pl.when(turn >= LAG_IN)
        def _():
            accumulate(turn - LAG_IN)

        return carry

    lax.fori_loop(0, steps + LAG_IN, inward, 0)

    gate = gate_acc[...]
    hidden[...] = (gate / (1.0 + jnp.exp(-gate)) * up_acc[...]).astype(BF16)

    def project(step):
        weight_load(2, step).wait()
        weight_send(2, step).wait_recv()
        half = down_v.shape[3]
        total = None
        for h in range(2):
            term = lax.dot_general(
                hidden[:, h * half : (h + 1) * half], down_v[step, h], (((1,), (1,)), ((), ())),
                preferred_element_type=F32,
            )
            total = term if total is None else total + term
        result = total.astype(BF16)
        made[step] = result
        back[step, :block] = result[:block]
        for across in range(2):
            for d in range(CUBE):
                if across + d > 0:
                    span = pl.ds((across * CUBE + d) * block, block)
                    send(
                        made.at[step, span], back.at[step, span], (s3.at[0, step], s3.at[1, step]),
                        near[d] if across else far[d], other if across else core,
                    )

    def combine(step):
        wait_for(back.at[step, pl.ds(block, slots - block)], s3.at[1, step])
        sums = dot(mix[...], back[step]).astype(BF16)
        part[step] = sums
        last[step, :count] = sums[:count]
        for d in range(1, CUBE):
            span = pl.ds(d * count, count)
            send(
                part.at[step, span], last.at[step, span], (s4.at[0, step], s4.at[1, step]),
                near[d], core,
            )

    def finish(step):
        wait_for(last.at[step, pl.ds(count, (CUBE - 1) * count)], s4.at[1, step])
        total = last[step, :count].astype(F32)
        for d in range(1, CUBE):
            total = total + last[step, d * count : (d + 1) * count].astype(F32)
        out[:, feature_span(step)] = total.astype(BF16)

    def outward(turn, carry):
        @pl.when(turn < steps)
        def _():
            project(turn)

        @pl.when((turn >= LAG_BACK) & (turn < steps + LAG_BACK))
        def _():
            combine(turn - LAG_BACK)

        @pl.when(turn >= LAG_SUM)
        def _():
            finish(turn - LAG_SUM)

        return carry

    lax.fori_loop(0, steps + LAG_SUM, outward, 0)

    wait_for(table.at[pl.ds(1, CUBE - 1)], table_sems.at[0])

    def drain(step, carry):
        wait_for(held.at[step, pl.ds(count, (CUBE - 1) * count)], s1.at[0, step])
        wait_for(sent.at[step, pl.ds(block, slots - block)], s2.at[0, step])
        wait_for(made.at[step, pl.ds(block, slots - block)], s3.at[0, step])
        wait_for(part.at[step, pl.ds(count, (CUBE - 1) * count)], s4.at[0, step])
        for which in range(3):
            weight_send(which, step).wait_send()
        return carry

    lax.fori_loop(0, steps, drain, 0)


def body(tokens, gate_weights, expert_ids, w_gate, w_up, w_down):
    count, features = tokens.shape
    units = w_gate.shape[2]
    steps = features // STEP
    gathered = CUBE * count
    slots = 2 * CUBE * CUBE * MOST
    dma = pltpu.SemaphoreType.DMA
    whole = pl.BlockSpec(memory_space=pl.ANY)
    vmem = pl.BlockSpec(memory_space=pltpu.VMEM)
    return pl.pallas_call(
        kernel,
        out_shape=jax.ShapeDtypeStruct((count, features), BF16),
        in_specs=[whole, vmem, vmem, whole, whole, whole],
        out_specs=vmem,
        scratch_shapes=[
            pltpu.VMEM((steps, gathered, STEP), BF16),
            pltpu.VMEM((CUBE, 2 * count, 128), BF16),
            pltpu.VMEM((slots, gathered), BF16),
            pltpu.VMEM((gathered, slots), BF16),
            pltpu.VMEM((steps, slots, STEP), BF16),
            pltpu.VMEM((steps, slots, STEP), BF16),
            pltpu.VMEM((slots, 2 * units), F32),
            pltpu.VMEM((slots, 2 * units), F32),
            pltpu.VMEM((slots, 2 * units), BF16),
            pltpu.VMEM((steps, slots, STEP), BF16),
            pltpu.VMEM((steps, slots, STEP), BF16),
            pltpu.VMEM((steps, gathered, STEP), BF16),
            pltpu.VMEM((steps, gathered, STEP), BF16),
            pltpu.VMEM((steps, 2, STEP, units), BF16),
            pltpu.VMEM((steps, 2, STEP, units), BF16),
            pltpu.VMEM((steps, 2, STEP, units), BF16),
            dma((steps,)),
            dma((2,)),
            dma((2, steps)),
            dma((2, steps)),
            dma((2, steps)),
            dma((2, steps)),
            dma((3, steps)),
            dma((3, steps)),
            dma((3, steps)),
        ],
        compiler_params=pltpu.CompilerParams(
            collective_id=0, has_side_effects=True, vmem_limit_bytes=66_000_000
        ),
    )(tokens, gate_weights, expert_ids, w_gate, w_up, w_down)


def solution(mesh):
    placed = (
        P(("grp", "loc"), None),
        P(("grp", "loc"), None),
        P(("grp", "loc"), None),
        P("grp", None, "loc"),
        P("grp", None, "loc"),
        P("grp", None, "loc"),
    )
    return jax.shard_map(
        body, mesh=mesh, in_specs=placed, out_specs=P(("grp", "loc"), None), check_vma=False
    )
```

time: 255 us -> 89.5 us (0.35)
  Pallas kernels: 0 us -> 84.9 us
  local copies, waits for them, and re-layouts: 62.1 us -> 4.36 us
  blocking collectives: 56.3 us -> 0 us
  waiting for transfers between devices: 46.5 us -> 0 us
  matrix products: 41.3 us -> 0 us
  starting transfers between devices: 22.4 us -> 0 us
  between operations: 13.3 us -> 0.01 us
  other arithmetic: 12.2 us -> 0 us
    pallas_call x0 -> x1, Pallas kernels: none -> 84.9 us  [body(): pl.pallas_call(kernel, out_shape=jax.ShapeDtypeStruct((count, features),...]
    all_to_all x1 -> x0, blocking collectives: 56.3 us -> none  [body(): lax.all_to_all(computed, 'grp', split_axis=0, concat_axis=0, tiled=True)]
    all_to_all x2 -> x0, waiting for transfers between devices: 44.4 us -> none  [the longest x1 44.4 us: body(): lax.all_to_all(send_rows, 'grp', split_axis=0, concat_axis=0, tiled=True)]
    dot_general x10 -> x0, matrix products: 41.3 us -> none  [the longest x4 28 us: expert_rows(): lax.dot_general(hidden, down_part, (((1,), (1,)), ((), ())), preferred_el...]
    squeeze x3 -> x0, local copies, waits for them, and re-layouts: 27.6 us -> none  [the longest x1 10.6 us: weights_path(): up_piece[expert][:, lower_unit:upper_unit]]
    all_to_all x2 -> x0, starting transfers between devices: 22.3 us -> none  [the longest x1 12 us: body(): lax.all_to_all(send_scales, 'grp', split_axis=0, concat_axis=0, tiled=True)]
    reshape x2 -> x0, local copies, waits for them, and re-layouts: 14.2 us -> none  [the longest x1 7.38 us: body(): send_rows.reshape(group_count, local_experts, slot_depth, feature_count)]
    another operation x4 -> x0, local copies, waits for them, and re-layouts: 13.2 us -> none  [the longest x2 7.44 us: weights_path(): jnp.stack([folded_part.reshape(row_dims[0], row_dims[2], row_dims[3]) for...]
  transfers between devices with their start and end apart: 5 -> 0, of which waited for: 1 -> 0; matrix products, arithmetic and copies ran while one was open for 19% -> 0% of each run, Pallas kernels for 0% -> 0%
where the time goes in v1:
time: 89.5 us; the launch traced here: 89.2 us
  Pallas kernels  84.9 us (95%)
  local copies, waits for them, and re-layouts  4.36 us (5%)
    pallas_call x1, Pallas kernels, body(): pl.pallas_call(kernel, out_shape=jax.ShapeDtypeStruct((count, features),...  84.9 us
    unnamed x3, local copies, waits for them, and re-layouts  4.36 us

profile of v1, /device:TPU:1, one launch (start us, length us, event | category | flops | bytes accessed | tf_op | source)
XLA Modules:
  0.0 89.2 jit_solution(3578857389180450655)
XLA Ops:
  0.0 1.4 %copy.7.scales = bf16[32,8]{1,0:T(8,128)(2,1)} copy(bf16[32,8]{0,1:T(8,128)(2,1)} %param.7) | data formatting | bytes 1024 | tf_op args[1]
  1.4 1.4 %copy.8.ids = s32[32,8]{1,0:T(8,128)} copy(s32[32,8]{0,1:T(8,128)} %param.8) | data formatting | bytes 2048 | tf_op args[2]
  2.7 84.9 %shard_map.64 = bf16[32,3584]{1,0:T(8,128)(2,1)} custom-call(bf16[32,3584]{1,0:T(8,128)(2,1)} %tokens.1, bf16[32,8]{1,0:T(8,128)(2,1)} %copy.7.scales, s32[32,8]{1,0:T(8,128)} %copy.8.ids, bf16[2,3584,512]{2,1,0:T(8,128)(2,1)} %w_gate.1, bf16[2,3584,512]{2,1,0:T(8,128)(2,1)} %w_up.1, bf16[2,3584,512]{2,1,0:T(8,128)(2,1)} %w_down.1), custom_call_target="tpu_custom_call" | custom-call | tf_op jit(solution)/shard_map/pallas_call | solution.py:293
  87.6 1.6 %copy.10 = bf16[32,3584]{1,0:T(8,128)(2,1)} copy(bf16[32,3584]{1,0:T(8,128)(2,1)} %shard_map.64) | data formatting | bytes 458752

commit v2 on v1

--- a/solution.py
+++ b/solution.py
@@ -9,9 +9,7 @@
 CUBE = 8
 MOST = 4
 STEP = 512
-LAG_IN = 2
-LAG_BACK = 3
-LAG_SUM = 5
+LAG_SUM = 3
 F32 = jnp.float32
 BF16 = jnp.bfloat16
 
@@ -31,6 +29,10 @@
 
 def dot(left, right):
     return jnp.dot(left, right, preferred_element_type=F32)
+
+
+def dot_t(left, right):
+    return lax.dot_general(left, right, (((1,), (1,)), ((), ())), preferred_element_type=F32)
 
 
 def kernel(
@@ -109,20 +111,20 @@
 
     lax.fori_loop(0, steps, start_weights, 0)
 
-    expert_line = lax.broadcasted_iota(jnp.int32, (count, 128), 1)
-    chosen = jnp.zeros((count, 128), F32)
-    weight_of = jnp.zeros((count, 128), F32)
-    for k in range(ids.shape[1]):
-        match = ids[:, k : k + 1] == expert_line
+    expert_row = lax.broadcasted_iota(jnp.int32, (128, count), 0)
+    chosen = jnp.zeros((128, count), F32)
+    weight_of = jnp.zeros((128, count), F32)
+    for k in range(ids.shape[0]):
+        match = ids[k : k + 1, :] == expert_row
         chosen = chosen + jnp.where(match, 1.0, 0.0)
-        weight_of = weight_of + jnp.where(match, scales[:, k : k + 1].astype(F32), 0.0)
-    before = (
-        lax.broadcasted_iota(jnp.int32, (count, count), 1)
-        < lax.broadcasted_iota(jnp.int32, (count, count), 0)
-    )
-    earlier = dot(jnp.where(before, 1.0, 0.0).astype(BF16), chosen.astype(BF16))
-    table[0, :count] = (chosen * (earlier + 1.0)).astype(BF16)
-    table[0, count:] = weight_of.astype(BF16)
+        weight_of = weight_of + jnp.where(match, scales[k : k + 1, :].astype(F32), 0.0)
+    column = lax.broadcasted_iota(jnp.int32, (count, count), 1)
+    row = lax.broadcasted_iota(jnp.int32, (count, count), 0)
+    same = jnp.where(column == row, 1.0, 0.0).astype(BF16)
+    before = jnp.where(column < row, 1.0, 0.0).astype(BF16)
+    chosen = chosen.astype(BF16)
+    table[0, :count] = (dot_t(same, chosen) * (dot_t(before, chosen) + 1.0)).astype(BF16)
+    table[0, count:] = dot_t(same, weight_of.astype(BF16)).astype(BF16)
     gate_acc[...] = jnp.zeros_like(gate_acc)
     up_acc[...] = jnp.zeros_like(up_acc)
 
@@ -165,74 +167,86 @@
     mix[...] = jnp.where(hit, dot(weights, widen), 0.0).astype(BF16)
     pick[...] = jnp.where(hit, 1.0, 0.0).T.astype(BF16)
 
+    def half_span(across):
+        low = across * CUBE * block
+        return pl.ds(low + block * (1 - across), CUBE * block - block * (1 - across))
+
+    def send_rows(across, step):
+        for d in range(across == 0, CUBE):
+            span = pl.ds((across * CUBE + d) * block, block)
+            send(
+                sent.at[step, span], rows.at[step, span],
+                (s2.at[0, across, step], s2.at[1, across, step]),
+                far[d], other if across else core,
+            )
+
     def select(step):
         wait_for(held.at[step, pl.ds(count, (CUBE - 1) * count)], s1.at[1, step])
         chosen_rows = dot(pick[...], held[step]).astype(BF16)
         sent[step] = chosen_rows
         rows[step, :block] = chosen_rows[:block]
-        for across in range(2):
-            for d in range(CUBE):
-                if across + d > 0:
-                    span = pl.ds((across * CUBE + d) * block, block)
-                    send(
-                        sent.at[step, span], rows.at[step, span], (s2.at[0, step], s2.at[1, step]),
-                        far[d], other if across else core,
-                    )
+        send_rows(0, step)
         for which in range(3):
             weight_send(which, step).start()
 
-    def accumulate(step):
-        for which in range(2):
-            weight_load(which, step).wait()
-            weight_send(which, step).wait_recv()
-        wait_for(rows.at[step, pl.ds(block, slots - block)], s2.at[1, step])
-        arrived = rows[step]
-        half = gate_v.shape[3]
-        for h in range(2):
-            gate_acc[:, h * half : (h + 1) * half] += dot(arrived, gate_v[step, h])
-            up_acc[:, h * half : (h + 1) * half] += dot(arrived, up_v[step, h])
-
-    def inward(turn, carry):
-        @pl.when(turn < steps)
-        def _():
-            select(turn)
-
-        @pl.when(turn >= LAG_IN)
-        def _():
-            accumulate(turn - LAG_IN)
-
-        return carry
-
-    lax.fori_loop(0, steps + LAG_IN, inward, 0)
-
-    gate = gate_acc[...]
-    hidden[...] = (gate / (1.0 + jnp.exp(-gate)) * up_acc[...]).astype(BF16)
-
-    def project(step):
-        weight_load(2, step).wait()
-        weight_send(2, step).wait_recv()
-        half = down_v.shape[3]
-        total = None
-        for h in range(2):
-            term = lax.dot_general(
-                hidden[:, h * half : (h + 1) * half], down_v[step, h], (((1,), (1,)), ((), ())),
-                preferred_element_type=F32,
-            )
-            total = term if total is None else total + term
-        result = total.astype(BF16)
-        made[step] = result
-        back[step, :block] = result[:block]
+    def inward(step, carry):
+        select(step)
+        return carry
+
+    lax.fori_loop(0, steps, inward, 0)
+
+    def second_half(step, carry):
+        send_rows(1, step)
+        return carry
+
+    lax.fori_loop(0, steps, second_half, 0)
+
+    half = gate_v.shape[3]
+    for across in range(2):
+        low = across * CUBE * block
+        these = slice(low, low + CUBE * block)
+
+        def accumulate(step, carry):
+            if across == 0:
+                for which in range(2):
+                    weight_load(which, step).wait()
+                    weight_send(which, step).wait_recv()
+            wait_for(rows.at[step, half_span(across)], s2.at[1, across, step])
+            arrived = rows[step, these]
+            for h in range(2):
+                gate_acc[these, h * half : (h + 1) * half] += dot(arrived, gate_v[step, h])
+                up_acc[these, h * half : (h + 1) * half] += dot(arrived, up_v[step, h])
+            return carry
+
+        lax.fori_loop(0, steps, accumulate, 0)
+        gate = gate_acc[these]
+        hidden[these] = (gate / (1.0 + jnp.exp(-gate)) * up_acc[these]).astype(BF16)
+
+        def project(step, carry):
+            if across == 0:
+                weight_load(2, step).wait()
+                weight_send(2, step).wait_recv()
+            result = (
+                dot_t(hidden[these, :half], down_v[step, 0])
+                + dot_t(hidden[these, half:], down_v[step, 1])
+            ).astype(BF16)
+            made[step, these] = result
+            if across == 0:
+                back[step, :block] = result[:block]
+            for d in range(across == 0, CUBE):
+                span = pl.ds((across * CUBE + d) * block, block)
+                send(
+                    made.at[step, span], back.at[step, span],
+                    (s3.at[0, across, step], s3.at[1, across, step]),
+                    near[d] if across else far[d], other if across else core,
+                )
+            return carry
+
+        lax.fori_loop(0, steps, project, 0)
+
+    def combine(step):
         for across in range(2):
-            for d in range(CUBE):
-                if across + d > 0:
-                    span = pl.ds((across * CUBE + d) * block, block)
-                    send(
-                        made.at[step, span], back.at[step, span], (s3.at[0, step], s3.at[1, step]),
-                        near[d] if across else far[d], other if across else core,
-                    )
-
-    def combine(step):
-        wait_for(back.at[step, pl.ds(block, slots - block)], s3.at[1, step])
+            wait_for(back.at[step, half_span(across)], s3.at[1, across, step])
         sums = dot(mix[...], back[step]).astype(BF16)
         part[step] = sums
         last[step, :count] = sums[:count]
@@ -253,11 +267,7 @@
     def outward(turn, carry):
         @pl.when(turn < steps)
         def _():
-            project(turn)
-
-        @pl.when((turn >= LAG_BACK) & (turn < steps + LAG_BACK))
-        def _():
-            combine(turn - LAG_BACK)
+            combine(turn)
 
         @pl.when(turn >= LAG_SUM)
         def _():
@@ -271,8 +281,9 @@
 
     def drain(step, carry):
         wait_for(held.at[step, pl.ds(count, (CUBE - 1) * count)], s1.at[0, step])
-        wait_for(sent.at[step, pl.ds(block, slots - block)], s2.at[0, step])
-        wait_for(made.at[step, pl.ds(block, slots - block)], s3.at[0, step])
+        for across in range(2):
+            wait_for(sent.at[step, half_span(across)], s2.at[0, across, step])
+            wait_for(made.at[step, half_span(across)], s3.at[0, across, step])
         wait_for(part.at[step, pl.ds(count, (CUBE - 1) * count)], s4.at[0, step])
         for which in range(3):
             weight_send(which, step).wait_send()
@@ -315,8 +326,8 @@
             dma((steps,)),
             dma((2,)),
             dma((2, steps)),
-            dma((2, steps)),
-            dma((2, steps)),
+            dma((2, 2, steps)),
+            dma((2, 2, steps)),
             dma((2, steps)),
             dma((3, steps)),
             dma((3, steps)),
@@ -325,7 +336,7 @@
         compiler_params=pltpu.CompilerParams(
             collective_id=0, has_side_effects=True, vmem_limit_bytes=66_000_000
         ),
-    )(tokens, gate_weights, expert_ids, w_gate, w_up, w_down)
+    )(tokens, gate_weights.T, expert_ids.T, w_gate, w_up, w_down)
 
 
 def solution(mesh):

time: 89.5 us -> 79.8 us (0.89)
  Pallas kernels: 84.9 us -> 78 us
  local copies, waits for them, and re-layouts: 4.36 us -> 1.64 us
    pallas_call x1, Pallas kernels: 84.9 us -> 78 us  [body(): pl.pallas_call(kernel, out_shape=jax.ShapeDtypeStruct((count, features),...]
    unnamed x3 -> x1, local copies, waits for them, and re-layouts: 4.36 us -> 1.64 us
where the time goes in v2:
time: 79.8 us; the launch traced here: 79.6 us
  Pallas kernels  78 us (98%)
  local copies, waits for them, and re-layouts  1.64 us (2%)
    pallas_call x1, Pallas kernels, body(): pl.pallas_call(kernel, out_shape=jax.ShapeDtypeStruct((count, features),...  78 us
    unnamed x1, local copies, waits for them, and re-layouts  1.64 us

profile of v2, /device:TPU:1, one launch (start us, length us, event | category | flops | bytes accessed | tf_op | source)
XLA Modules:
  0.0 79.6 jit_solution(6296235707216244489)
XLA Ops:
  0.0 78.0 %shard_map.64 = bf16[32,3584]{1,0:T(8,128)(2,1)} custom-call(bf16[32,3584]{1,0:T(8,128)(2,1)} %tokens.1, bf16[8,32]{1,0:T(8,128)(2,1)} %bitcast.3, s32[8,32]{1,0:T(8,128)} %bitcast.2, bf16[2,3584,512]{2,1,0:T(8,128)(2,1)} %w_gate.1, bf16[2,3584,512]{2,1,0:T(8,128)(2,1)} %w_up.1, bf16[2,3584,512]{2,1,0:T(8,128)(2,1)} %w_down.1), custom_call_target="tpu_custom_call" | custom-call | tf_op jit(solution)/shard_map/pallas_call | solution.py:304
  78.0 1.6 %copy.8 = bf16[32,3584]{1,0:T(8,128)(2,1)} copy(bf16[32,3584]{1,0:T(8,128)(2,1)} %shard_map.64) | data formatting | bytes 458752

commit v3 on v2

--- a/solution.py
+++ b/solution.py
@@ -8,8 +8,10 @@
 SIDE = 4
 CUBE = 8
 MOST = 4
-STEP = 512
-LAG_SUM = 3
+STEP = 896
+ORDER = (7, 3, 5, 6, 1, 2, 4)
+ONE_AWAY = (1, 2, 4)
+ON = (2, 4, 1)
 F32 = jnp.float32
 BF16 = jnp.bfloat16
 
@@ -37,7 +39,7 @@
 
 def kernel(
     tokens, scales, ids, w_gate, w_up, w_down, out,
-    held, table, pick, mix, sent, rows, gate_acc, up_acc, hidden, made, back, part, last,
+    held, table, pick, mix, sent, rows, gate_acc, up_acc, hidden, made, back, part, last, moved,
     gate_v, up_v, down_v,
     tok_sem, table_sems, s1, s2, s3, s4, w_local, w_send, w_recv,
 ):
@@ -91,6 +93,13 @@
 
     def wait_for(ref, sem):
         pltpu.make_async_copy(ref, ref, sem).wait()
+
+    def pass_tokens(step, block_here, block_there, chip, phase):
+        send(
+            held.at[step, pl.ds(block_here * count, count)],
+            held.at[step, pl.ds(block_there * count, count)],
+            (s1.at[0, phase, step], s1.at[1, phase, step]), chip, core,
+        )
 
     for step in range(steps):
         token_load(step).start()
@@ -130,19 +139,20 @@
 
     pl.semaphore_wait(barrier, len(partners))
 
-    for d in range(1, CUBE):
-        send(table.at[0], table.at[d], (table_sems.at[0], table_sems.at[1]), near[d], core)
-
-    def spread(step, carry):
+    for step in range(steps):
         token_load(step).wait()
-        for d in range(1, CUBE):
-            send(
-                held.at[step, pl.ds(0, count)], held.at[step, pl.ds(d * count, count)],
-                (s1.at[0, step], s1.at[1, step]), near[d], core,
-            )
-        return carry
-
-    lax.fori_loop(0, steps, spread, 0)
+        for d in ONE_AWAY:
+            pass_tokens(step, 0, d, near[d], 0)
+        if step == 0:
+            for d in ORDER:
+                send(table.at[0], table.at[d], (table_sems.at[0], table_sems.at[1]), near[d], core)
+
+    for step in range(steps):
+        wait_for(held.at[step, pl.ds(0, len(ONE_AWAY) * count)], s1.at[1, 0, step])
+        via = step % len(ONE_AWAY)
+        pass_tokens(step, ONE_AWAY[via], 7, near[7 - ONE_AWAY[via]], 1)
+        for d, along in zip(ONE_AWAY, ON):
+            pass_tokens(step, d, d + along, near[along], 1)
 
     slot = lax.broadcasted_iota(jnp.int32, (1, slots), 1)
     slot_core = slot // (CUBE * block)
@@ -172,7 +182,7 @@
         return pl.ds(low + block * (1 - across), CUBE * block - block * (1 - across))
 
     def send_rows(across, step):
-        for d in range(across == 0, CUBE):
+        for d in ORDER + (0,) * across:
             span = pl.ds((across * CUBE + d) * block, block)
             send(
                 sent.at[step, span], rows.at[step, span],
@@ -181,7 +191,7 @@
             )
 
     def select(step):
-        wait_for(held.at[step, pl.ds(count, (CUBE - 1) * count)], s1.at[1, step])
+        wait_for(held.at[step, pl.ds(0, (len(ONE_AWAY) + 1) * count)], s1.at[1, 1, step])
         chosen_rows = dot(pick[...], held[step]).astype(BF16)
         sent[step] = chosen_rows
         rows[step, :block] = chosen_rows[:block]
@@ -233,7 +243,7 @@
             made[step, these] = result
             if across == 0:
                 back[step, :block] = result[:block]
-            for d in range(across == 0, CUBE):
+            for d in ORDER + (0,) * across:
                 span = pl.ds((across * CUBE + d) * block, block)
                 send(
                     made.at[step, span], back.at[step, span],
@@ -244,47 +254,58 @@
 
         lax.fori_loop(0, steps, project, 0)
 
-    def combine(step):
+    def pass_sums(source, step, block_here, block_there, chip, phase):
+        send(
+            source.at[step, pl.ds(block_here * count, count)],
+            last.at[step, pl.ds(block_there * count, count)],
+            (s4.at[0, phase, step], s4.at[1, phase, step]), chip, core,
+        )
+
+    def combine(step, carry):
         for across in range(2):
             wait_for(back.at[step, half_span(across)], s3.at[1, across, step])
         sums = dot(mix[...], back[step]).astype(BF16)
         part[step] = sums
-        last[step, :count] = sums[:count]
-        for d in range(1, CUBE):
-            span = pl.ds(d * count, count)
-            send(
-                part.at[step, span], last.at[step, span], (s4.at[0, step], s4.at[1, step]),
-                near[d], core,
-            )
-
-    def finish(step):
-        wait_for(last.at[step, pl.ds(count, (CUBE - 1) * count)], s4.at[1, step])
-        total = last[step, :count].astype(F32)
-        for d in range(1, CUBE):
+        via = lax.rem(step, len(ONE_AWAY))
+        pass_sums(part, step, 7, 7, jnp.where(via == 0, near[6], jnp.where(via == 1, near[5], near[3])), 0)
+        for d, along in zip(ONE_AWAY, ON):
+            pass_sums(part, step, d + along, d + along, near[along], 0)
+        return carry
+
+    def relay(step, carry):
+        wait_for(last.at[step, pl.ds(0, (len(ONE_AWAY) + 1) * count)], s4.at[1, 0, step])
+        via = lax.rem(step, len(ONE_AWAY))
+        farthest = last[step, 7 * count :].astype(F32)
+        for k, (d, along) in enumerate(zip(ONE_AWAY, ON)):
+            here = pl.ds(d * count, count)
+            total = part[step, here].astype(F32) + last[step, pl.ds((d + along) * count, count)].astype(F32)
+            moved[step, here] = (total + jnp.where(via == k, farthest, 0.0)).astype(BF16)
+        for d in ONE_AWAY:
+            pass_sums(moved, step, d, d, near[d], 1)
+        return carry
+
+    def finish(step, carry):
+        wait_for(last.at[step, pl.ds(0, len(ONE_AWAY) * count)], s4.at[1, 1, step])
+        total = part[step, :count].astype(F32)
+        for d in ONE_AWAY:
             total = total + last[step, d * count : (d + 1) * count].astype(F32)
         out[:, feature_span(step)] = total.astype(BF16)
-
-    def outward(turn, carry):
-        @pl.when(turn < steps)
-        def _():
-            combine(turn)
-
-        @pl.when(turn >= LAG_SUM)
-        def _():
-            finish(turn - LAG_SUM)
-
-        return carry
-
-    lax.fori_loop(0, steps + LAG_SUM, outward, 0)
+        return carry
+
+    lax.fori_loop(0, steps, combine, 0)
+    lax.fori_loop(0, steps, relay, 0)
+    lax.fori_loop(0, steps, finish, 0)
 
     wait_for(table.at[pl.ds(1, CUBE - 1)], table_sems.at[0])
 
     def drain(step, carry):
-        wait_for(held.at[step, pl.ds(count, (CUBE - 1) * count)], s1.at[0, step])
+        for phase in range(2):
+            moved_rows = pl.ds(0, (len(ONE_AWAY) + 1 - phase) * count)
+            wait_for(held.at[step, pl.ds(0, (len(ONE_AWAY) + phase) * count)], s1.at[0, phase, step])
+            wait_for(part.at[step, moved_rows], s4.at[0, phase, step])
         for across in range(2):
             wait_for(sent.at[step, half_span(across)], s2.at[0, across, step])
             wait_for(made.at[step, half_span(across)], s3.at[0, across, step])
-        wait_for(part.at[step, pl.ds(count, (CUBE - 1) * count)], s4.at[0, step])
         for which in range(3):
             weight_send(which, step).wait_send()
         return carry
@@ -320,15 +341,16 @@
             pltpu.VMEM((steps, slots, STEP), BF16),
             pltpu.VMEM((steps, gathered, STEP), BF16),
             pltpu.VMEM((steps, gathered, STEP), BF16),
+            pltpu.VMEM((steps, gathered, STEP), BF16),
             pltpu.VMEM((steps, 2, STEP, units), BF16),
             pltpu.VMEM((steps, 2, STEP, units), BF16),
             pltpu.VMEM((steps, 2, STEP, units), BF16),
             dma((steps,)),
             dma((2,)),
-            dma((2, steps)),
             dma((2, 2, steps)),
             dma((2, 2, steps)),
-            dma((2, steps)),
+            dma((2, 2, steps)),
+            dma((2, 2, steps)),
             dma((3, steps)),
             dma((3, steps)),
             dma((3, steps)),

time: 79.8 us -> 73.9 us (0.926)
  Pallas kernels: 78 us -> 72.1 us
    pallas_call x1, Pallas kernels: 78 us -> 72.1 us  [body(): pl.pallas_call(kernel, out_shape=jax.ShapeDtypeStruct((count, features),...]
where the time goes in v3:
time: 73.9 us; the launch traced here: 73.8 us
  Pallas kernels  72.1 us (98%)
  local copies, waits for them, and re-layouts  1.64 us (2%)
    pallas_call x1, Pallas kernels, body(): pl.pallas_call(kernel, out_shape=jax.ShapeDtypeStruct((count, features),...  72.1 us
    unnamed x1, local copies, waits for them, and re-layouts  1.64 us

profile of v3, /device:TPU:1, one launch (start us, length us, event | category | flops | bytes accessed | tf_op | source)
XLA Modules:
  0.0 73.8 jit_solution(2412368583522309836)
XLA Ops:
  0.0 72.1 %shard_map.64 = bf16[32,3584]{1,0:T(8,128)(2,1)} custom-call(bf16[32,3584]{1,0:T(8,128)(2,1)} %tokens.1, bf16[8,32]{1,0:T(8,128)(2,1)} %bitcast.3, s32[8,32]{1,0:T(8,128)} %bitcast.2, bf16[2,3584,512]{2,1,0:T(8,128)(2,1)} %w_gate.1, bf16[2,3584,512]{2,1,0:T(8,128)(2,1)} %w_up.1, bf16[2,3584,512]{2,1,0:T(8,128)(2,1)} %w_down.1), custom_call_target="tpu_custom_call" | custom-call | tf_op jit(solution)/shard_map/pallas_call | solution.py:325
  72.1 1.6 %copy.8 = bf16[32,3584]{1,0:T(8,128)(2,1)} copy(bf16[32,3584]{1,0:T(8,128)(2,1)} %shard_map.64) | data formatting | bytes 458752

commit v4 on v3

--- a/solution.py
+++ b/solution.py
@@ -38,9 +38,9 @@
 
 
 def kernel(
-    tokens, scales, ids, w_gate, w_up, w_down, out,
+    tokens, scales_in, ids_in, w_gate, w_up, w_down, out,
     held, table, pick, mix, sent, rows, gate_acc, up_acc, hidden, made, back, part, last, moved,
-    gate_v, up_v, down_v,
+    gate_v, up_v, down_v, scales, ids, small_sem,
     tok_sem, table_sems, s1, s2, s3, s4, w_local, w_send, w_recv,
 ):
     count = tokens.shape[0]
@@ -103,6 +103,12 @@
 
     for step in range(steps):
         token_load(step).start()
+    small_loads = [
+        pltpu.make_async_copy(ids_in, ids, small_sem.at[0]),
+        pltpu.make_async_copy(scales_in, scales, small_sem.at[1]),
+    ]
+    for load in small_loads:
+        load.start()
     barrier = pltpu.get_barrier_semaphore()
     partners = [(me, other)]
     for d in range(1, CUBE):
@@ -120,6 +126,8 @@
 
     lax.fori_loop(0, steps, start_weights, 0)
 
+    for load in small_loads:
+        load.wait()
     expert_row = lax.broadcasted_iota(jnp.int32, (128, count), 0)
     chosen = jnp.zeros((128, count), F32)
     weight_of = jnp.zeros((128, count), F32)
@@ -315,6 +323,7 @@
 
 def body(tokens, gate_weights, expert_ids, w_gate, w_up, w_down):
     count, features = tokens.shape
+    choices = expert_ids.shape[1]
     units = w_gate.shape[2]
     steps = features // STEP
     gathered = CUBE * count
@@ -324,8 +333,8 @@
     vmem = pl.BlockSpec(memory_space=pltpu.VMEM)
     return pl.pallas_call(
         kernel,
-        out_shape=jax.ShapeDtypeStruct((count, features), BF16),
-        in_specs=[whole, vmem, vmem, whole, whole, whole],
+        out_shape=pltpu.VMEM((count, features), BF16),
+        in_specs=[whole, whole, whole, whole, whole, whole],
         out_specs=vmem,
         scratch_shapes=[
             pltpu.VMEM((steps, gathered, STEP), BF16),
@@ -345,6 +354,9 @@
             pltpu.VMEM((steps, 2, STEP, units), BF16),
             pltpu.VMEM((steps, 2, STEP, units), BF16),
             pltpu.VMEM((steps, 2, STEP, units), BF16),
+            pltpu.VMEM((choices, count), BF16),
+            pltpu.VMEM((choices, count), jnp.int32),
+            dma((2,)),
             dma((steps,)),
             dma((2,)),
             dma((2, 2, steps)),
@@ -356,9 +368,9 @@
             dma((3, steps)),
         ],
         compiler_params=pltpu.CompilerParams(
-            collective_id=0, has_side_effects=True, vmem_limit_bytes=66_000_000
+            collective_id=0, has_side_effects=True, vmem_limit_bytes=54_000_000
         ),
-    )(tokens, gate_weights.T, expert_ids.T, w_gate, w_up, w_down)
+    )(*(pltpu.with_memory_space_constraint(x, pltpu.HBM) for x in (tokens, gate_weights.T, expert_ids.T, w_gate, w_up, w_down)))
 
 
 def solution(mesh):

time: 73.9 us -> 71.6 us (0.969)
  Pallas kernels: 72.1 us -> 70.8 us
  local copies, waits for them, and re-layouts: 1.64 us -> 0.69 us
    pallas_call x1, Pallas kernels: 72.1 us -> 70.8 us  [body(): pl.pallas_call(kernel, out_shape=pltpu.VMEM((count, features), BF16), in_...]
    unnamed x1, local copies, waits for them, and re-layouts: 1.64 us -> 0.69 us
where the time goes in v4:
time: 71.6 us; the launch traced here: 71.5 us
  Pallas kernels  70.8 us (99%)
    pallas_call x1, Pallas kernels, body(): pl.pallas_call(kernel, out_shape=pltpu.VMEM((count, features), BF16), in_...  70.8 us

profile of v4, /device:TPU:1, one launch (start us, length us, event | category | flops | bytes accessed | tf_op | source)
XLA Modules:
  0.0 71.5 jit_solution(9145788306188756971)
XLA Ops:
  0.0 70.8 %shard_map.64 = bf16[32,3584]{1,0:T(8,128)(2,1)S(1)} custom-call(bf16[32,3584]{1,0:T(8,128)(2,1)} %tokens.1, bf16[8,32]{1,0:T(8,128)(2,1)} %bitcast.3, s32[8,32]{1,0:T(8,128)} %bitcast.2, bf16[2,3584,512]{2,1,0:T(8,128)(2,1)} %w_gate.1, bf16[2,3584,512]{2,1,0:T(8,128)(2,1)} %w_up.1, bf16[2,3584,512]{2,1,0:T(8,128)(2,1)} %w_down.1), custom_call_target="tpu_custom_call" | custom-call | tf_op jit(solution)/shard_map/pallas_call | solution.py:334
  70.8 0.7 copy.8

commit v5 on v4

--- a/solution.py
+++ b/solution.py
@@ -40,7 +40,7 @@
 def kernel(
     tokens, scales_in, ids_in, w_gate, w_up, w_down, out,
     held, table, pick, mix, sent, rows, gate_acc, up_acc, hidden, made, back, part, last, moved,
-    gate_v, up_v, down_v, scales, ids, small_sem,
+    gate_v, up_v, down_v, scales, ids, ready, small_sem,
     tok_sem, table_sems, s1, s2, s3, s4, w_local, w_send, w_recv,
 ):
     count = tokens.shape[0]
@@ -109,15 +109,20 @@
     ]
     for load in small_loads:
         load.start()
+    neighbours = [(me, other)] + [(cube[d], core) for cube in (near, far) for d in ONE_AWAY]
+
+    def greet(semaphore):
+        for chip, to_core in neighbours:
+            pl.semaphore_signal(
+                semaphore, inc=1, device_id={"grp": chip, "loc": to_core},
+                device_id_type=pl.DeviceIdType.MESH,
+            )
+
+    def greeted(semaphore):
+        pl.semaphore_wait(semaphore, len(neighbours))
+
     barrier = pltpu.get_barrier_semaphore()
-    partners = [(me, other)]
-    for d in range(1, CUBE):
-        partners += [(near[d], core), (near[d], other), (far[d], core), (far[d], other)]
-    for chip, to_core in partners:
-        pl.semaphore_signal(
-            barrier, inc=1, device_id={"grp": chip, "loc": to_core},
-            device_id_type=pl.DeviceIdType.MESH,
-        )
+    greet(barrier)
 
     def start_weights(step, carry):
         for which in range(3):
@@ -126,6 +131,26 @@
 
     lax.fori_loop(0, steps, start_weights, 0)
 
+    greeted(barrier)
+    greet(ready.at[0])
+
+    def pass_table(block_here, block_there, chip, phase):
+        send(
+            table.at[block_here], table.at[block_there],
+            (table_sems.at[0, phase], table_sems.at[1, phase]), chip, core,
+        )
+
+    def pass_on(step):
+        wait_for(held.at[step, pl.ds(0, len(ONE_AWAY) * count)], s1.at[1, 0, step])
+        via = step % len(ONE_AWAY)
+        pass_tokens(step, ONE_AWAY[via], 7, near[7 - ONE_AWAY[via]], 1)
+        for d, along in zip(ONE_AWAY, ON):
+            pass_tokens(step, d, d + along, near[along], 1)
+
+    for step in range(steps):
+        token_load(step).wait()
+        for d in ONE_AWAY:
+            pass_tokens(step, 0, d, near[d], 0)
     for load in small_loads:
         load.wait()
     expert_row = lax.broadcasted_iota(jnp.int32, (128, count), 0)
@@ -145,22 +170,20 @@
     gate_acc[...] = jnp.zeros_like(gate_acc)
     up_acc[...] = jnp.zeros_like(up_acc)
 
-    pl.semaphore_wait(barrier, len(partners))
-
-    for step in range(steps):
-        token_load(step).wait()
-        for d in ONE_AWAY:
-            pass_tokens(step, 0, d, near[d], 0)
-        if step == 0:
-            for d in ORDER:
-                send(table.at[0], table.at[d], (table_sems.at[0], table_sems.at[1]), near[d], core)
-
-    for step in range(steps):
-        wait_for(held.at[step, pl.ds(0, len(ONE_AWAY) * count)], s1.at[1, 0, step])
-        via = step % len(ONE_AWAY)
-        pass_tokens(step, ONE_AWAY[via], 7, near[7 - ONE_AWAY[via]], 1)
-        for d, along in zip(ONE_AWAY, ON):
-            pass_tokens(step, d, d + along, near[along], 1)
+    for d in ONE_AWAY:
+        pass_table(0, d, near[d], 0)
+    greeted(ready.at[0])
+    greet(ready.at[1])
+    pass_on(0)
+    pass_on(1)
+    wait_for(table.at[pl.ds(0, len(ONE_AWAY))], table_sems.at[1, 0])
+    pass_table(1, 7, near[6], 1)
+    for d, along in zip(ONE_AWAY, ON):
+        pass_table(d, d + along, near[along], 1)
+    greeted(ready.at[1])
+    greet(ready.at[2])
+    for step in range(2, steps):
+        pass_on(step)
 
     slot = lax.broadcasted_iota(jnp.int32, (1, slots), 1)
     slot_core = slot // (CUBE * block)
@@ -177,13 +200,15 @@
         lax.broadcasted_iota(jnp.int32, (128, slots), 0) == slot_expert, 1.0, 0.0
     ).astype(BF16)
 
-    wait_for(table.at[pl.ds(1, CUBE - 1)], table_sems.at[1])
+    wait_for(table.at[pl.ds(0, len(ONE_AWAY) + 1)], table_sems.at[1, 1])
     codes = jnp.concatenate([table[d, :count] for d in range(CUBE)], axis=0)
     weights = jnp.concatenate([table[d, count:] for d in range(CUBE)], axis=0)
     token_source = lax.broadcasted_iota(jnp.int32, (CUBE * count, 1), 0) // count
     hit = (dot(codes, widen) == (slot_rank + 1).astype(F32)) & (token_source == slot_source)
     mix[...] = jnp.where(hit, dot(weights, widen), 0.0).astype(BF16)
     pick[...] = jnp.where(hit, 1.0, 0.0).T.astype(BF16)
+
+    greeted(ready.at[2])
 
     def half_span(across):
         low = across * CUBE * block
@@ -304,7 +329,8 @@
     lax.fori_loop(0, steps, relay, 0)
     lax.fori_loop(0, steps, finish, 0)
 
-    wait_for(table.at[pl.ds(1, CUBE - 1)], table_sems.at[0])
+    for phase in range(2):
+        wait_for(table.at[pl.ds(0, len(ONE_AWAY) + phase)], table_sems.at[0, phase])
 
     def drain(step, carry):
         for phase in range(2):
@@ -356,9 +382,10 @@
             pltpu.VMEM((steps, 2, STEP, units), BF16),
             pltpu.VMEM((choices, count), BF16),
             pltpu.VMEM((choices, count), jnp.int32),
+            pltpu.SemaphoreType.REGULAR((3,)),
             dma((2,)),
             dma((steps,)),
-            dma((2,)),
+            dma((2, 2)),
             dma((2, 2, steps)),
             dma((2, 2, steps)),
             dma((2, 2, steps)),

time: 71.6 us -> 68.7 us (0.959)
  Pallas kernels: 70.8 us -> 67.9 us
    pallas_call x1, Pallas kernels: 70.8 us -> 67.9 us  [body(): pl.pallas_call(kernel, out_shape=pltpu.VMEM((count, features), BF16), in_...]
where the time goes in v5:
time: 68.7 us; the launch traced here: 68.6 us
  Pallas kernels  67.9 us (99%)
  local copies, waits for them, and re-layouts  0.69 us (1%)
    pallas_call x1, Pallas kernels, body(): pl.pallas_call(kernel, out_shape=pltpu.VMEM((count, features), BF16), in_...  67.9 us

profile of v5, /device:TPU:1, one launch (start us, length us, event | category | flops | bytes accessed | tf_op | source)
XLA Modules:
  0.0 68.6 jit_solution(4434454779416159858)
XLA Ops:
  0.0 67.9 %shard_map.64 = bf16[32,3584]{1,0:T(8,128)(2,1)S(1)} custom-call(bf16[32,3584]{1,0:T(8,128)(2,1)} %tokens.1, bf16[8,32]{1,0:T(8,128)(2,1)} %bitcast.3, s32[8,32]{1,0:T(8,128)} %bitcast.2, bf16[2,3584,512]{2,1,0:T(8,128)(2,1)} %w_gate.1, bf16[2,3584,512]{2,1,0:T(8,128)(2,1)} %w_up.1, bf16[2,3584,512]{2,1,0:T(8,128)(2,1)} %w_down.1), custom_call_target="tpu_custom_call" | custom-call | tf_op jit(solution)/shard_map/pallas_call | solution.py:360
  67.9 0.7 %copy.8 = bf16[32,3584]{1,0:T(8,128)(2,1)} copy(bf16[32,3584]{1,0:T(8,128)(2,1)S(1)} %shard_map.64) | data formatting | bytes 458752

commit v6 on v5

--- a/solution.py
+++ b/solution.py
@@ -8,7 +8,8 @@
 SIDE = 4
 CUBE = 8
 MOST = 4
-STEP = 896
+DIRECT = 1
+STEP = 512
 ORDER = (7, 3, 5, 6, 1, 2, 4)
 ONE_AWAY = (1, 2, 4)
 ON = (2, 4, 1)
@@ -124,12 +125,6 @@
     barrier = pltpu.get_barrier_semaphore()
     greet(barrier)
 
-    def start_weights(step, carry):
-        for which in range(3):
-            weight_load(which, step).start()
-        return carry
-
-    lax.fori_loop(0, steps, start_weights, 0)
 
     greeted(barrier)
     greet(ready.at[0])
@@ -151,6 +146,13 @@
         token_load(step).wait()
         for d in ONE_AWAY:
             pass_tokens(step, 0, d, near[d], 0)
+    def start_weights(step, carry):
+        for which in range(3):
+            weight_load(which, step).start()
+        return carry
+
+    lax.fori_loop(0, steps, start_weights, 0)
+
     for load in small_loads:
         load.wait()
     expert_row = lax.broadcasted_iota(jnp.int32, (128, count), 0)
@@ -287,6 +289,8 @@
 
         lax.fori_loop(0, steps, project, 0)
 
+    relayed = steps - DIRECT
+
     def pass_sums(source, step, block_here, block_there, chip, phase):
         send(
             source.at[step, pl.ds(block_here * count, count)],
@@ -300,9 +304,19 @@
         sums = dot(mix[...], back[step]).astype(BF16)
         part[step] = sums
         via = lax.rem(step, len(ONE_AWAY))
-        pass_sums(part, step, 7, 7, jnp.where(via == 0, near[6], jnp.where(via == 1, near[5], near[3])), 0)
-        for d, along in zip(ONE_AWAY, ON):
-            pass_sums(part, step, d + along, d + along, near[along], 0)
+
+        @pl.when(step < relayed)
+        def _():
+            corner = jnp.where(via == 0, near[6], jnp.where(via == 1, near[5], near[3]))
+            pass_sums(part, step, 7, 7, corner, 0)
+            for d, along in zip(ONE_AWAY, ON):
+                pass_sums(part, step, d + along, d + along, near[along], 0)
+
+        @pl.when(step >= relayed)
+        def _():
+            for d in ORDER:
+                pass_sums(part, step, d, d, near[d], 0)
+
         return carry
 
     def relay(step, carry):
@@ -326,8 +340,18 @@
         return carry
 
     lax.fori_loop(0, steps, combine, 0)
-    lax.fori_loop(0, steps, relay, 0)
-    lax.fori_loop(0, steps, finish, 0)
+    lax.fori_loop(0, relayed, relay, 0)
+
+    def finish_direct(step, carry):
+        wait_for(last.at[step, pl.ds(count, (CUBE - 1) * count)], s4.at[1, 0, step])
+        total = part[step, :count].astype(F32)
+        for d in range(1, CUBE):
+            total = total + last[step, d * count : (d + 1) * count].astype(F32)
+        out[:, feature_span(step)] = total.astype(BF16)
+        return carry
+
+    lax.fori_loop(0, relayed, finish, 0)
+    lax.fori_loop(relayed, steps, finish_direct, 0)
 
     for phase in range(2):
         wait_for(table.at[pl.ds(0, len(ONE_AWAY) + phase)], table_sems.at[0, phase])
@@ -336,7 +360,15 @@
         for phase in range(2):
             moved_rows = pl.ds(0, (len(ONE_AWAY) + 1 - phase) * count)
             wait_for(held.at[step, pl.ds(0, (len(ONE_AWAY) + phase) * count)], s1.at[0, phase, step])
-            wait_for(part.at[step, moved_rows], s4.at[0, phase, step])
+
+            @pl.when(step < relayed)
+            def _():
+                wait_for(part.at[step, moved_rows], s4.at[0, phase, step])
+
+        @pl.when(step >= relayed)
+        def _():
+            wait_for(part.at[step, pl.ds(count, (CUBE - 1) * count)], s4.at[0, 0, step])
+
         for across in range(2):
             wait_for(sent.at[step, half_span(across)], s2.at[0, across, step])
             wait_for(made.at[step, half_span(across)], s3.at[0, across, step])

time: 68.7 us -> 68.9 us (level)
  no operation moved by 1% of the time
where the time goes in v6:
time: 68.9 us; the launch traced here: 68.8 us
  Pallas kernels  68.1 us (99%)
  local copies, waits for them, and re-layouts  0.69 us (1%)
    pallas_call x1, Pallas kernels, body(): pl.pallas_call(kernel, out_shape=pltpu.VMEM((count, features), BF16), in_...  68.1 us

profile of v6, /device:TPU:1, one launch (start us, length us, event | category | flops | bytes accessed | tf_op | source)
XLA Modules:
  0.0 68.8 jit_solution(8551927787454392576)
XLA Ops:
  0.0 68.1 %shard_map.64 = bf16[32,3584]{1,0:T(8,128)(2,1)S(1)} custom-call(bf16[32,3584]{1,0:T(8,128)(2,1)} %tokens.1, bf16[8,32]{1,0:T(8,128)(2,1)} %bitcast.3, s32[8,32]{1,0:T(8,128)} %bitcast.2, bf16[2,3584,512]{2,1,0:T(8,128)(2,1)} %w_gate.1, bf16[2,3584,512]{2,1,0:T(8,128)(2,1)} %w_up.1, bf16[2,3584,512]{2,1,0:T(8,128)(2,1)} %w_down.1), custom_call_target="tpu_custom_call" | custom-call | tf_op jit(solution)/shard_map/pallas_call | solution.py:392
  68.1 0.7 %copy.8 = bf16[32,3584]{1,0:T(8,128)(2,1)} copy(bf16[32,3584]{1,0:T(8,128)(2,1)S(1)} %shard_map.64) | data formatting | bytes 458752
